TPU v7x, 128 devices: a whole 4x4x4 slice. The times are simulated.
128 devices in a mesh: row: 16 (over z, x), col: 8 (over y, core).
Axes of the slice: x: 4, y: 4, z: 4, core: 2. Of those that a mesh axis runs over, the one named last changes fastest.
Arguments:
- density_first: bfloat16 [12288, 12288], P('row', 'col'), may hold values from -0.0068359375 to 0.0068359375
- density_second: bfloat16 [12288, 12288], P('row', 'col'), may hold values from -0.0068359375 to 0.0068359375
- basis: bfloat16 [256, 4096, 896], P(('row', 'col')), may hold values from -6 to 6
- tile_list: int32 [256, 7], P(('row', 'col')), may hold values from 0 to 95, as said below
- tile_count: int32 [256], P(('row', 'col')), may hold values from 5 to 7, as said below
- point_count: int32 [256], P(('row', 'col')), may hold values from 1024 to 4096, as said below
- offsets: float32 [3, 256, 4096], P(None, ('row', 'col')), may hold values from -5 to 5
- weights: float32 [256, 4096], P(('row', 'col')), may hold values from 0.05 to 1
- atom_of_point: int32 [256, 4096], P(('row', 'col')), may hold values from 0 to 1023, as said below
Outputs:
- density: float32 [2, 256, 4096], P(None, ('row', 'col'))
- moments: float32 [2, 9, 1024], replicated
Inputs may be any that keep to these rules, and one draw needn't show every extreme that they name: `tile_list`: the 7 tile numbers of each batch are 7 consecutive numbers in some order. `tile_count`: some batch has 7. `point_count`: some batch has 4096. `atom_of_point`: the points of batch g belong to atoms (g * 4 + j) mod 1024 with j from 0 to 7.
All inputs are finite; a program needn't handle non-finite values.
Results may differ from a plain program's by a relative error of at most 0.0003.
Values may be sent and summed in bfloat16 or wider, within the bound.
A program may use at most 192 MiB of HBM per device.

v0:
```python
import functools

import jax
import jax.numpy as jnp
from jax import lax
from jax.experimental import pallas as pl
from jax.experimental.pallas import tpu as pltpu
from jax.sharding import Mesh
from jax.sharding import PartitionSpec as P

TILE = 128
ATOMS = 1024
ROW = ("row_0", "row_1")
COL = ("col_0", "col_1")
ROW_COL = ("row_0", "row_1", "col_0", "col_1")
KT = 7
N_ROW = 16
N_COL = 8
DEVS = N_ROW * N_COL
NT = 96
STARTS = NT - KT + 1
LOCAL_T = NT // N_ROW
LOCAL_U = NT // N_COL
BLOCK = 512
GROUPS = BLOCK // TILE
F32 = jnp.float32
BF16 = jnp.bfloat16
I16 = jnp.int16
I32 = jnp.int32
VMEM_LIMIT = 60 * 1024 * 1024
SMEM_SPEC = pl.BlockSpec(memory_space=pltpu.SMEM)
VMEM_SPEC = pl.BlockSpec(memory_space=pltpu.VMEM)
ANY_SPEC = pl.BlockSpec(memory_space=pl.ANY)


def extract_kernel(meta, first, second, out, tiles, sems):
    r = meta[0]
    c = meta[1]
    e = lax.bitwise_and(c - r, 7)

    def fetch(m, ul, t):
        column = r + 16 * t + e - 8 * ul - c
        column = jnp.clip(lax.shift_right_arithmetic(column, 3), 0, LOCAL_U - 1)
        source = (first, second)[m]
        return pltpu.make_async_copy(
            source.at[pl.ds(t * TILE, TILE), pl.ds(pl.multiple_of(column * TILE, TILE), TILE)],
            tiles.at[m, ul, t],
            sems.at[m, ul, t],
        )

    todo = [(m, ul, t) for m in range(2) for ul in range(2) for t in range(LOCAL_T)]
    for item in todo:
        fetch(*item).start()
    out[...] = jnp.zeros(out.shape, out.dtype)
    for m, ul, t in todo:
        fetch(m, ul, t).wait()
        row_tile = r + 16 * t
        d = e if ul == 0 else 8 - e
        near = d <= 3
        if ul == 0:
            key = jnp.where(near, row_tile, row_tile + d)
            turned = (e >= 1) & (e <= 3)
        else:
            key = jnp.where(near, row_tile - d, row_tile)
            turned = e <= 4
        kind = jnp.where(near, d, 7 - d)
        q = lax.bitwise_and(kind + 4 * m + lax.shift_right_arithmetic(key, 4), 7)
        tile = tiles[m, ul, t].astype(F32)
        tile = jnp.where(turned, tile.T, tile)
        out[:, q, m, ul] = tile.reshape(N_ROW, 8, TILE).astype(BF16)


def extract(meta, first, second):
    return pl.pallas_call(
        extract_kernel,
        name="extract",
        out_shape=jax.ShapeDtypeStruct((N_ROW, N_COL, 2, 2, 8, TILE), BF16),
        in_specs=[SMEM_SPEC, ANY_SPEC, ANY_SPEC],
        out_specs=VMEM_SPEC,
        scratch_shapes=[
            pltpu.VMEM((2, 2, LOCAL_T, TILE, TILE), BF16),
            pltpu.SemaphoreType.DMA((2, 2, LOCAL_T)),
        ],
        compiler_params=pltpu.CompilerParams(vmem_limit_bytes=VMEM_LIMIT),
    )(meta, first, second)


def encode(value):
    size = jnp.abs(value)
    safe = jnp.maximum(size, 2.0**-38)
    power = jnp.floor(jnp.log2(safe))
    code = (power + 37.0) * 1024.0 + safe * jnp.exp2(10.0 - power)
    code = jnp.clip(jnp.floor(code + 0.5), 0.0, 32767.0)
    code = jnp.where(size >= 2.0**-38, code, 0.0)
    code = jnp.where(value < 0.0, -code, code)
    return code.astype(I32).astype(I16)


def decode(code):
    code = code.astype(I32)
    size = jnp.abs(code)
    power = lax.shift_right_logical(size, 10).astype(F32)
    fraction = (lax.bitwise_and(size, 1023) + 1024).astype(F32)
    value = fraction * jnp.exp2(power - 48.0)
    value = jnp.where(size > 0, value, 0.0)
    return jnp.where(code < 0, -value, value)


def pack_kernel(meta, starts, slices, out, table, windows, sem):
    q = meta[1]

    def kind_of(k):
        return lax.bitwise_and(q - lax.shift_right_arithmetic(k, 4), 7)

    def fill(k, carry):
        which = kind_of(k)
        kind = lax.bitwise_and(which, 3)
        m = lax.shift_right_arithmetic(which, 2)

        def owner(row_tile, col_tile):
            return lax.bitwise_and(row_tile, 15) * 8 + lax.bitwise_and(col_tile, 7)

        far = k + kind
        upper = slices[owner(k, far), m, 0].astype(F32)
        lower = slices[owner(far, k), m, 1].astype(F32)
        table[2 * k] = encode(jnp.where(kind > 0, upper + lower, upper))
        near = k - 7 + kind
        upper = slices[owner(near, k), m, 0].astype(F32)
        lower = slices[owner(k, near), m, 1].astype(F32)
        table[2 * k + 1] = encode(upper + lower)
        return carry

    lax.fori_loop(0, NT, fill, 0, unroll=4)

    def window(a, carry):
        for t in range(KT):
            kind = lax.bitwise_and(kind_of(a + t), 3)
            wraps = (kind > 0) & (t + kind > KT - 1)
            windows[a, t] = table[2 * (a + t) + wraps.astype(I32)]
        return carry

    lax.fori_loop(0, STARTS, window, 0, unroll=2)

    def send(d, carry):
        for b in range(2):
            pltpu.make_async_copy(windows.at[starts[2 * d + b]], out.at[b, d], sem).start()
        return carry

    lax.fori_loop(0, DEVS, send, 0, unroll=4)
    pltpu.make_async_copy(out, out, sem).wait()


def pack(meta, starts, slices):
    return pl.pallas_call(
        pack_kernel,
        name="pack",
        out_shape=jax.ShapeDtypeStruct((2, DEVS, KT, 8, TILE), I16),
        in_specs=[SMEM_SPEC, SMEM_SPEC, VMEM_SPEC],
        out_specs=ANY_SPEC,
        scratch_shapes=[
            pltpu.VMEM((2 * NT, 8, TILE), I16),
            pltpu.VMEM((STARTS, KT, 8, TILE), I16),
            pltpu.SemaphoreType.DMA,
        ],
        compiler_params=pltpu.CompilerParams(vmem_limit_bytes=VMEM_LIMIT),
    )(meta, starts, slices)


def harmonics(x, y, z):
    radius_sq = x * x + y * y + z * z
    return [
        None,
        x,
        y,
        z,
        x * y,
        y * z,
        3.0 * z * z - radius_sq,
        x * z,
        x * x - y * y,
    ]


def batch_kernel(
    batch, info, arrived, basis, offsets, weights, atoms, dens, moments, matrix, phi, sums, sems
):
    start = info[0]
    count = info[1]
    base = info[2]
    blocks = lax.div(count + (BLOCK - 1), BLOCK)

    def fetch(block, slot, j):
        place = pl.multiple_of(info[3 + j % KT] * TILE, TILE)
        return pltpu.make_async_copy(
            basis.at[batch, pl.ds(pl.multiple_of(block * BLOCK, BLOCK), BLOCK), pl.ds(place, TILE)],
            phi.at[slot, :, pl.ds(j * TILE, TILE)],
            sems.at[slot, j],
        )

    for j in range(KT + 3):
        fetch(0, 0, j).start()

    for t in range(KT):
        turn = lax.shift_right_arithmetic(start + t, 4)
        for kind in range(4):
            live = (info[10 + t] * info[10 + (t + kind) % KT]).astype(F32)
            for m in range(2):
                q = lax.bitwise_and(kind + 4 * m + turn, 7)
                value = decode(arrived[:, q, t]).reshape(TILE, TILE) * live
                high = value.astype(BF16)
                low = (value - high.astype(F32)).astype(BF16)
                columns = pl.ds(m * TILE, TILE)
                matrix[t, pl.ds(kind * TILE, TILE), columns] = high
                matrix[t, pl.ds((4 + kind) * TILE, TILE), columns] = low

    dens[...] = jnp.zeros(dens.shape, F32)

    def step(block, carry):
        slot = lax.bitwise_and(block, 1)

        @pl.when(block + 1 < blocks)
        def _():
            for j in range(KT + 3):
                fetch(block + 1, 1 - slot, j).start()

        for j in range(KT + 3):
            fetch(block, slot, j).wait()
        total = jnp.zeros((BLOCK, 2 * TILE), F32)
        for t in range(KT):
            left = phi[slot, :, pl.ds(t * TILE, 4 * TILE)]
            product = jnp.dot(
                left, matrix[t, pl.ds(0, 4 * TILE), :], preferred_element_type=F32
            ) + jnp.dot(left, matrix[t, pl.ds(4 * TILE, 4 * TILE), :], preferred_element_type=F32)
            own = left[:, :TILE].astype(F32)
            total = total + product * jnp.concatenate([own, own], axis=1)
        for m in range(2):
            for i in range(GROUPS):
                part = total[i * TILE : (i + 1) * TILE, m * TILE : (m + 1) * TILE]
                dens[m, pl.ds(block * GROUPS + i, 1), :] = jnp.sum(part.T, axis=0, keepdims=True)
        return carry

    lax.fori_loop(0, blocks, step, 0)

    rows = dens.shape[1]
    place = lax.broadcasted_iota(I32, (rows, TILE), 0) * TILE + lax.broadcasted_iota(
        I32, (rows, TILE), 1
    )
    inside = place < count
    harmonic = harmonics(offsets[0], offsets[1], offsets[2])
    weight = weights[...]
    factors = [weight] + [weight * item for item in harmonic[1:]]
    hits = [atoms[...] == lax.bitwise_and(base + j, ATOMS - 1) for j in range(8)]
    sums[...] = jnp.zeros(sums.shape, F32)
    for m in range(2):
        value = jnp.where(inside, dens[m], 0.0)
        dens[m] = value
        for h in range(9):
            term = value * factors[h]
            for j in range(8):
                picked = jnp.where(hits[j], term, 0.0)
                sums[pl.ds(j * 18 + m * 9 + h, 1), :] = jnp.sum(picked, axis=0, keepdims=True)
    for i in range(2):
        part = sums[pl.ds(i * TILE, TILE), :]
        moments[pl.ds(i, 1), :] = jnp.sum(part.T, axis=0, keepdims=True)


def batch_density(batch, info, arrived, basis, offsets, weights, atoms):
    points = basis.shape[1]
    rows = points // TILE
    return pl.pallas_call(
        functools.partial(batch_kernel, batch),
        name="batch_density",
        out_shape=(
            jax.ShapeDtypeStruct((2, rows, TILE), F32),
            jax.ShapeDtypeStruct((2, TILE), F32),
        ),
        in_specs=[SMEM_SPEC, VMEM_SPEC, ANY_SPEC, VMEM_SPEC, VMEM_SPEC, VMEM_SPEC],
        out_specs=(VMEM_SPEC, VMEM_SPEC),
        scratch_shapes=[
            pltpu.VMEM((KT, 8 * TILE, 2 * TILE), BF16),
            pltpu.VMEM((2, BLOCK, (KT + 3) * TILE), BF16),
            pltpu.VMEM((2 * TILE, TILE), F32),
            pltpu.SemaphoreType.DMA((2, KT + 3)),
        ],
        compiler_params=pltpu.CompilerParams(vmem_limit_bytes=VMEM_LIMIT),
        cost_estimate=pl.CostEstimate(
            flops=2 * points * 1024 * 256 * KT, bytes_accessed=12_000_000, transcendentals=0
        ),
    )(info, arrived, basis, offsets, weights, atoms)


def exchange(value):
    return lax.all_to_all(value, ROW_COL, split_axis=0, concat_axis=0, tiled=True)


def local(
    density_first,
    density_second,
    basis,
    tile_list,
    tile_count,
    point_count,
    offsets,
    weights,
    atom_of_point,
):
    points = basis.shape[1]
    rows = points // TILE
    my_row = lax.axis_index(ROW).astype(I32)
    my_col = lax.axis_index(COL).astype(I32)
    device = my_row * N_COL + my_col
    meta = jnp.stack([my_row, my_col])
    own_start = jnp.min(tile_list, axis=1)
    starts = exchange(jnp.broadcast_to(own_start[None], (DEVS, 2))).reshape(-1)

    slices = extract(meta, density_first, density_second)
    slices = exchange(slices.reshape(DEVS, 2, 2, 8, TILE))
    outgoing = pack(meta, starts, slices)
    arrived = [exchange(outgoing[b]) for b in range(2)]

    place = jnp.argsort(tile_list, axis=1).astype(I32)
    live = (place < tile_count[:, None]).astype(I32)
    base = (2 * device + jnp.arange(2, dtype=I32)) * 4 % ATOMS
    info = jnp.concatenate(
        [own_start[:, None], point_count[:, None], base[:, None], place, live], axis=1
    )
    dens = []
    moments = []
    for b in range(2):
        one, part = batch_density(
            b,
            info[b],
            arrived[b].reshape(N_ROW, N_COL, KT, 8, TILE),
            basis,
            offsets[:, b].reshape(3, rows, TILE),
            weights[b].reshape(rows, TILE),
            atom_of_point[b].reshape(rows, TILE),
        )
        dens.append(one.reshape(2, points))
        moments.append(part.reshape(-1)[: 8 * 18])
    density = jnp.stack(dens, axis=1)
    half = 4 * 18
    own = jnp.concatenate(
        [moments[0][:half], moments[0][half:] + moments[1][:half], moments[1][half:]]
    )
    spare = jnp.zeros((2 * TILE - 3 * half,), F32)
    own = jnp.concatenate([own, spare])
    everyone = exchange(jnp.broadcast_to(own[None], (DEVS, 2 * TILE)))
    main = everyone[:, : 2 * half]
    extra = jnp.roll(everyone[:, 2 * half : 3 * half], 1, axis=0)
    whole = main + jnp.concatenate([extra, jnp.zeros_like(extra)], axis=1)
    whole = whole.reshape(ATOMS, 18).T.reshape(2, 9, ATOMS)
    return (density, whole)


def solution(mesh):
    torus = Mesh(mesh.devices.reshape(4, 4, 4, 2), ("row_0", "row_1", "col_0", "col_1"))
    in_specs = (
        P(ROW, COL),
        P(ROW, COL),
        P(ROW_COL, None, None),
        P(ROW_COL, None),
        P(ROW_COL),
        P(ROW_COL),
        P(None, ROW_COL, None),
        P(ROW_COL, None),
        P(ROW_COL, None),
    )
    out_specs = (P(None, ROW_COL, None), P())
    return jax.shard_map(local, mesh=torus, in_specs=in_specs, out_specs=out_specs, check_vma=False)
```

profile of v0, /device:TPU:1, one launch (start us, length us, event | category | flops | bytes accessed | tf_op | source)
XLA Modules:
  0.0 167.2 jit_solution(8360367026292597777)
XLA Ops:
  0.6 0.8 reduce_min.9
  1.4 0.7 broadcast_in_dim.12
  2.1 11.5 %all-to-all-start = ((s32[128,1,2]{2,1,0:T(1,128)}), s32[128,1,2]{2,1,0:T(1,128)S(1)}, u32[]{:S(2)}, u32[]{:S(2)}) async-start(s32[128,1,2]{2,1,0:T(1,128)} %broadcast_in_dim.12), calls=%async_computation | async-start | bytes 131072 | tf_op jit(solution)/shard_map/all_to_all | solution.py:293
  13.6 0.6 pad_add_fusion.meta
  14.2 5.1 %extract.1 = bf16[16,8,2,2,8,128]{5,4,3,2,1,0:T(8,128)(2,1)} custom-call(s32[2]{0:T(128)} %pad_add_fusion.meta, bf16[768,1536]{1,0:T(8,128)(2,1)} %first.1, bf16[768,1536]{1,0:T(8,128)(2,1)} %second.1), custom_call_target="tpu_custom_call" | custom-call | tf_op jit(solution)/shard_map/extract/pallas_call | solution.py:74
  19.3 3.8 %all-to-all-done = s32[128,1,2]{2,1,0:T(1,128)S(1)} async-done(((s32[128,1,2]{2,1,0:T(1,128)}), s32[128,1,2]{2,1,0:T(1,128)S(1)}, u32[]{:S(2)}, u32[]{:S(2)}) %all-to-all-start) | async-done | bytes 1056 | tf_op jit(solution)/shard_map/all_to_all | solution.py:293
  23.1 5.9 %all-to-all-start.1 = ((bf16[128,2,2,8,128]{4,3,2,1,0:T(8,128)(2,1)}), bf16[128,2,2,8,128]{4,3,2,1,0:T(8,128)(2,1)S(1)}, u32[]{:S(2)}, u32[]{:S(2)}) async-start(bf16[128,2,2,8,128]{4,3,2,1,0:T(8,128)(2,1)} %bitcast.29), calls=%async_computation.1 | async-start | bytes 2097152 | tf_op jit(solution)/shard_map/all_to_all | solution.py:293
  29.1 0.5 broadcast.79
  29.6 0.8 reduce.3
  30.4 0.7 reshape.85.starts
  31.1 16.8 %all-to-all-done.1.slices = bf16[128,2,2,8,128]{4,3,2,1,0:T(8,128)(2,1)S(1)} async-done(((bf16[128,2,2,8,128]{4,3,2,1,0:T(8,128)(2,1)}), bf16[128,2,2,8,128]{4,3,2,1,0:T(8,128)(2,1)S(1)}, u32[]{:S(2)}, u32[]{:S(2)}) %all-to-all-start.1) | async-done | bytes 1048608 | tf_op jit(solution)/shard_map/all_to_all | solution.py:293
  47.9 1.0 copy-done
  48.9 6.1 %pack.1 = s16[2,128,7,8,128]{4,3,2,1,0:T(8,128)(2,1)} custom-call(s32[2]{0:T(128)} %pad_add_fusion.meta, s32[256]{0:T(256)} %reshape.85.starts, bf16[128,2,2,8,128]{4,3,2,1,0:T(8,128)(2,1)} %copy-done), custom_call_target="tpu_custom_call" | custom-call | tf_op jit(solution)/shard_map/pack/pallas_call | solution.py:154
  55.0 4.5 %slice_bitcast_fusion.1 = (s16[128,7,8,128]{3,2,1,0:T(8,128)(2,1)}, s16[128,7,8,128]{3,2,1,0:T(8,128)(2,1)}) fusion(s16[2,128,7,8,128]{4,3,2,1,0:T(8,128)(2,1)} %pack.1), kind=kLoop, calls=%fused_computation.1 | loop fusion | bytes 7340032 | tf_op jit(solution)/shard_map/squeeze | solution.py:319
  59.5 4.9 %all-to-all-start.3 = ((s16[128,7,8,128]{3,2,1,0:T(8,128)(2,1)}), s16[128,7,8,128]{3,2,1,0:T(8,128)(2,1)S(1)}, u32[]{:S(2)}, u32[]{:S(2)}) async-start(s16[128,7,8,128]{3,2,1,0:T(8,128)(2,1)} %get-tuple-element.19), calls=%async_computation.3 | async-start | bytes 3670016 | tf_op jit(solution)/shard_map/all_to_all | solution.py:293
  64.4 0.0 copy-done.3
  64.5 0.6 fusion.4
  65.1 0.0 copy-done.6
  65.1 0.1 copy.25
  65.2 0.7 sort.17
  65.8 0.0 copy-done.4
  65.8 0.6 fusion.3
  66.5 0.0 copy-done.2
  66.5 0.7 fusion.2
  67.2 24.6 %all-to-all-done.3 = s16[128,7,8,128]{3,2,1,0:T(8,128)(2,1)S(1)} async-done(((s16[128,7,8,128]{3,2,1,0:T(8,128)(2,1)}), s16[128,7,8,128]{3,2,1,0:T(8,128)(2,1)S(1)}, u32[]{:S(2)}, u32[]{:S(2)}) %all-to-all-start.3) | async-done | bytes 1835040 | tf_op jit(solution)/shard_map/all_to_all | solution.py:293
  91.8 1.2 copy-done.1
  93.1 5.8 %all-to-all-start.2 = ((s16[128,7,8,128]{3,2,1,0:T(8,128)(2,1)}), s16[128,7,8,128]{3,2,1,0:T(8,128)(2,1)}, u32[]{:S(2)}, u32[]{:S(2)}) async-start(s16[128,7,8,128]{3,2,1,0:T(8,128)(2,1)} %get-tuple-element.18), calls=%async_computation.2 | async-start | bytes 3670016 | tf_op jit(solution)/shard_map/all_to_all | solution.py:293
  98.9 0.0 copy-done.8
  98.9 0.1 copy.28
  99.0 0.1 copy.26
  99.1 0.1 copy.27
  99.2 0.1 copy.29
  99.3 0.1 concatenate.13
  99.4 0.6 slice_bitcast_fusion.3
  100.0 16.5 %batch_density.3 = (f32[2,32,128]{2,1,0:T(8,128)}, f32[2,128]{1,0:T(2,128)}) custom-call(s32[17]{0:T(128)} %get-tuple-element.30.info, s16[16,8,7,8,128]{4,3,2,1,0:T(8,128)(2,1)} %bitcast.31, bf16[2,4096,896]{2,1,0:T(8,128)(2,1)} %basis.3, f32[3,32,128]{2,1,0:T(8,128)} %bitcast.36, f32[32,128]{1,0:T(8,128)} %bitcast.41, s32[32,128]{1,0:T(8,128)} %bitcast.42), custom_call_target="tpu_custom_call" | custom-call | flops 15032385536 | bytes 12000000 | tf_op jit(solution)/shard_map/batch_density/pallas_call | solution.py:270
  116.5 9.4 %all-to-all-done.2 = s16[128,7,8,128]{3,2,1,0:T(8,128)(2,1)} async-done(((s16[128,7,8,128]{3,2,1,0:T(8,128)(2,1)}), s16[128,7,8,128]{3,2,1,0:T(8,128)(2,1)}, u32[]{:S(2)}, u32[]{:S(2)}) %all-to-all-start.2) | async-done | bytes 1835040 | tf_op jit(solution)/shard_map/all_to_all | solution.py:293
  125.9 18.5 %batch_density.2 = (f32[2,32,128]{2,1,0:T(8,128)}, f32[2,128]{1,0:T(2,128)}) custom-call(s32[17]{0:T(128)} %get-tuple-element.29.info, s16[16,8,7,8,128]{4,3,2,1,0:T(8,128)(2,1)} %bitcast.7.arrived, bf16[2,4096,896]{2,1,0:T(8,128)(2,1)} %basis.3, f32[3,32,128]{2,1,0:T(8,128)} %bitcast.35, f32[32,128]{1,0:T(8,128)} %bitcast.39, s32[32,128]{1,0:T(8,128)} %bitcast.40), custom_call_target="tpu_custom_call" | custom-call | flops 15032385536 | bytes 12000000 | tf_op jit(solution)/shard_map/batch_density/pallas_call | solution.py:270
  144.5 0.8 fusion.5
  145.3 0.1 pad_maximum_fusion.1
  145.4 0.7 broadcast_in_dim.28
  146.1 9.7 %all-to-all-start.4 = ((f32[128,1,256]{2,1,0:T(1,128)}), f32[128,1,256]{2,1,0:T(1,128)S(1)}, u32[]{:S(2)}, u32[]{:S(2)}) async-start(f32[128,1,256]{2,1,0:T(1,128)} %broadcast_in_dim.28), calls=%async_computation.4 | async-start | bytes 262144 | tf_op jit(solution)/shard_map/all_to_all | solution.py:293
  155.8 1.5 pad_maximum_fusion
  157.3 8.6 %all-to-all-done.4 = f32[128,1,256]{2,1,0:T(1,128)S(1)} async-done(((f32[128,1,256]{2,1,0:T(1,128)}), f32[128,1,256]{2,1,0:T(1,128)S(1)}, u32[]{:S(2)}, u32[]{:S(2)}) %all-to-all-start.4) | async-done | bytes 131104 | tf_op jit(solution)/shard_map/all_to_all | solution.py:293
  165.9 0.1 slice.83
  165.9 0.1 slice.82
  166.0 0.2 reshape.91
  166.2 0.2 copy.32
  166.5 0.7 copy.33
  (20 shorter events, 0.1 us)
Async XLA Ops:
  2.1 21.1 %all-to-all-start = ((s32[128,1,2]{2,1,0:T(1,128)}), s32[128,1,2]{2,1,0:T(1,128)S(1)}, u32[]{:S(2)}, u32[]{:S(2)}) async-start(s32[128,1,2]{2,1,0:T(1,128)} %broadcast_in_dim.12), calls=%async_computation | async-start | bytes 131072 | tf_op jit(solution)/shard_map/all_to_all | solution.py:293
  23.1 24.7 %all-to-all-start.1 = ((bf16[128,2,2,8,128]{4,3,2,1,0:T(8,128)(2,1)}), bf16[128,2,2,8,128]{4,3,2,1,0:T(8,128)(2,1)S(1)}, u32[]{:S(2)}, u32[]{:S(2)}) async-start(bf16[128,2,2,8,128]{4,3,2,1,0:T(8,128)(2,1)} %bitcast.29), calls=%async_computation.1 | async-start | bytes 2097152 | tf_op jit(solution)/shard_map/all_to_all | solution.py:293
  47.9 1.0 copy-start
  59.5 5.0 %copy-start.3 = (f32[2,4096]{1,0:T(2,128)S(1)}, f32[2,4096]{1,0:T(2,128)}, u32[]{:S(2)}) copy-start(f32[2,4096]{1,0:T(2,128)} %param.16) | copy-start | bytes 98308
  59.5 5.6 %copy-start.6 = (s32[2,7]{1,0:T(2,128)S(1)}, s32[2,7]{1,0:T(2,128)}, u32[]{:S(2)}) copy-start(s32[2,7]{1,0:T(2,128)} %param.12) | copy-start | bytes 172
  59.5 6.3 %copy-start.4 = (s32[2,4096]{1,0:T(2,128)S(1)}, s32[2,4096]{1,0:T(2,128)}, u32[]{:S(2)}) copy-start(s32[2,4096]{1,0:T(2,128)} %param.17) | copy-start | bytes 98308
  59.5 7.0 %copy-start.2 = (f32[3,2,4096]{2,1,0:T(2,128)S(1)}, f32[3,2,4096]{2,1,0:T(2,128)}, u32[]{:S(2)}) copy-start(f32[3,2,4096]{2,1,0:T(2,128)} %param.15) | copy-start | bytes 294916
  59.5 32.3 %all-to-all-start.3 = ((s16[128,7,8,128]{3,2,1,0:T(8,128)(2,1)}), s16[128,7,8,128]{3,2,1,0:T(8,128)(2,1)S(1)}, u32[]{:S(2)}, u32[]{:S(2)}) async-start(s16[128,7,8,128]{3,2,1,0:T(8,128)(2,1)} %get-tuple-element.19), calls=%async_computation.3 | async-start | bytes 3670016 | tf_op jit(solution)/shard_map/all_to_all | solution.py:293
  91.8 1.3 copy-start.1
  91.8 7.1 %copy-start.8 = (s32[2]{0:T(128)S(1)}, s32[2]{0:T(128)}, u32[]{:S(2)}) copy-start(s32[2]{0:T(128)} %param.13) | copy-start | bytes 28
  91.8 7.3 %copy-start.9 = (s32[2]{0:T(128)S(1)}, s32[2]{0:T(128)}, u32[]{:S(2)}) copy-start(s32[2]{0:T(128)} %param.14) | copy-start | bytes 28
  93.1 32.9 %all-to-all-start.2 = ((s16[128,7,8,128]{3,2,1,0:T(8,128)(2,1)}), s16[128,7,8,128]{3,2,1,0:T(8,128)(2,1)}, u32[]{:S(2)}, u32[]{:S(2)}) async-start(s16[128,7,8,128]{3,2,1,0:T(8,128)(2,1)} %get-tuple-element.18), calls=%async_computation.2 | async-start | bytes 3670016 | tf_op jit(solution)/shard_map/all_to_all | solution.py:293
  125.9 18.6 %copy-start.7 = (f32[2,128]{1,0:T(2,128)S(1)}, f32[2,128]{1,0:T(2,128)}, u32[]{:S(2)}) copy-start(f32[2,128]{1,0:T(2,128)} %get-tuple-element.11) | copy-start | bytes 3076
  125.9 29.9 %copy-start.5 = (f32[2,32,128]{2,1,0:T(8,128)S(1)}, f32[2,32,128]{2,1,0:T(8,128)}, u32[]{:S(2)}) copy-start(f32[2,32,128]{2,1,0:T(8,128)} %get-tuple-element.9) | copy-start | bytes 98308
  146.1 19.7 %all-to-all-start.4 = ((f32[128,1,256]{2,1,0:T(1,128)}), f32[128,1,256]{2,1,0:T(1,128)S(1)}, u32[]{:S(2)}, u32[]{:S(2)}) async-start(f32[128,1,256]{2,1,0:T(1,128)} %broadcast_in_dim.28), calls=%async_computation.4 | async-start | bytes 262144 | tf_op jit(solution)/shard_map/all_to_all | solution.py:293
where the time goes:
time: 169 us; the launch traced here: 167 us
  waiting for transfers between devices  63.2 us (37%)
  Pallas kernels  46.3 us (27%)
  starting transfers between devices  37.9 us (22%)
  local copies, waits for them, and re-layouts  13.7 us (8%)
  other arithmetic  5.21 us (3%)
    all_to_all x5, waiting for transfers between devices, exchange(): lax.all_to_all(value, ROW_COL, split_axis=0, concat_axis=0, tiled=True)  63.2 us
    all_to_all x5, starting transfers between devices, exchange(): lax.all_to_all(value, ROW_COL, split_axis=0, concat_axis=0, tiled=True)  37.9 us
    pallas_call x2, Pallas kernels, batch_density(): pl.pallas_call(functools.partial(batch_kernel, batch), name='batch_densit...  35.1 us
    pallas_call x1, Pallas kernels, pack(): pl.pallas_call(pack_kernel, name='pack', out_shape=jax.ShapeDtypeStruct((...  6.14 us
    pallas_call x1, Pallas kernels, extract(): pl.pallas_call(extract_kernel, name='extract', out_shape=jax.ShapeDtypeSt...  5.11 us
    squeeze x1, local copies, waits for them, and re-layouts, local(): arrived = [exchange(outgoing[b]) for b in range(2)]  4.47 us
  transfers between devices with their start and end apart: 5, of which 5 were waited for; matrix products, arithmetic and copies ran while one was open for 5% of the time, Pallas kernels for 13%

commit v1 on v0

--- a/solution.py
+++ b/solution.py
@@ -106,6 +106,122 @@
     return jnp.where(code < 0, -value, value)
 
 
+MESH_ID = pl.DeviceIdType.MESH
+
+
+def position():
+    return [lax.axis_index(name) for name in ROW_COL]
+
+
+def flat(spot):
+    return ((spot[0] * 4 + spot[1]) * 4 + spot[2]) * 2 + spot[3]
+
+
+def partner(spot, i):
+    j = (i * 37) % DEVS
+    away = [j // 32, (j // 8) % 4, (j // 2) % 4, j % 2]
+    return [(p + o) % n for p, o, n in zip(spot, away, (4, 4, 4, 2), strict=True)]
+
+
+def wait_all(ref, sem):
+    pltpu.make_async_copy(ref, ref, sem).wait()
+
+
+def spread_kernel(slices, own, out, starts, send_sems, recv_sems, here_sems):
+    spot = position()
+    me = flat(spot)
+    mine = pltpu.make_async_copy(own, starts.at[me], here_sems.at[0])
+    mine.start()
+    kept = pltpu.make_async_copy(slices.at[me], out.at[me], here_sems.at[1])
+    kept.start()
+
+    def send_start(i, carry):
+        pltpu.make_async_remote_copy(
+            src_ref=own,
+            dst_ref=starts.at[me],
+            send_sem=send_sems.at[0],
+            recv_sem=recv_sems.at[0],
+            device_id=tuple(partner(spot, i)),
+            device_id_type=MESH_ID,
+        ).start()
+        return carry
+
+    def send_slices(i, carry):
+        to = partner(spot, i)
+        pltpu.make_async_remote_copy(
+            src_ref=slices.at[flat(to)],
+            dst_ref=out.at[me],
+            send_sem=send_sems.at[1],
+            recv_sem=recv_sems.at[1],
+            device_id=tuple(to),
+            device_id_type=MESH_ID,
+        ).start()
+        return carry
+
+    lax.fori_loop(1, DEVS, send_start, 0)
+    lax.fori_loop(1, DEVS, send_slices, 0)
+    mine.wait()
+    kept.wait()
+    others = pl.ds(0, DEVS - 1)
+    wait_all(starts.at[others], send_sems.at[0])
+    wait_all(starts.at[others], recv_sems.at[0])
+    wait_all(out.at[others], send_sems.at[1])
+    wait_all(out.at[others], recv_sems.at[1])
+
+
+def spread(slices, own):
+    return pl.pallas_call(
+        spread_kernel,
+        name="spread",
+        out_shape=(
+            jax.ShapeDtypeStruct(slices.shape, slices.dtype),
+            jax.ShapeDtypeStruct((DEVS, *own.shape), own.dtype),
+        ),
+        in_specs=[ANY_SPEC, ANY_SPEC],
+        out_specs=(ANY_SPEC, ANY_SPEC),
+        scratch_shapes=[pltpu.SemaphoreType.DMA((2,))] * 3,
+        compiler_params=pltpu.CompilerParams(
+            has_side_effects=True, vmem_limit_bytes=VMEM_LIMIT
+        ),
+    )(slices, own)
+
+
+def share_kernel(own, out, send_sem, recv_sem, here_sem):
+    spot = position()
+    me = flat(spot)
+    mine = pltpu.make_async_copy(own, out.at[me], here_sem)
+    mine.start()
+
+    def send(i, carry):
+        pltpu.make_async_remote_copy(
+            src_ref=own,
+            dst_ref=out.at[me],
+            send_sem=send_sem,
+            recv_sem=recv_sem,
+            device_id=tuple(partner(spot, i)),
+            device_id_type=MESH_ID,
+        ).start()
+        return carry
+
+    lax.fori_loop(1, DEVS, send, 0)
+    mine.wait()
+    others = pl.ds(0, DEVS - 1)
+    wait_all(out.at[others], send_sem)
+    wait_all(out.at[others], recv_sem)
+
+
+def share(own):
+    return pl.pallas_call(
+        share_kernel,
+        name="share",
+        out_shape=jax.ShapeDtypeStruct((DEVS, *own.shape), own.dtype),
+        in_specs=[ANY_SPEC],
+        out_specs=ANY_SPEC,
+        scratch_shapes=[pltpu.SemaphoreType.DMA] * 3,
+        compiler_params=pltpu.CompilerParams(has_side_effects=True, vmem_limit_bytes=VMEM_LIMIT),
+    )(own)
+
+
 def pack_kernel(meta, starts, slices, out, table, windows, sem):
     q = meta[1]
 
@@ -181,116 +297,155 @@
     ]
 
 
-def batch_kernel(
-    batch, info, arrived, basis, offsets, weights, atoms, dens, moments, matrix, phi, sums, sems
-):
-    start = info[0]
-    count = info[1]
-    base = info[2]
-    blocks = lax.div(count + (BLOCK - 1), BLOCK)
-
-    def fetch(block, slot, j):
-        place = pl.multiple_of(info[3 + j % KT] * TILE, TILE)
+CHUNKS = ((0, 0, 7), (1, 0, 4), (1, 4, 7))
+
+
+def batches_kernel(info, outgoing, basis, offsets, weights, atoms, dens, moments, *scratch):
+    arrived = scratch[: len(CHUNKS)]
+    values = scratch[len(CHUNKS) : len(CHUNKS) + 2]
+    matrix, kept, sums, send_sems, recv_sems, here_sems, basis_sems = scratch[len(CHUNKS) + 2 :]
+    spot = position()
+    me = flat(spot)
+    points = basis.shape[1]
+
+    def own_copy(n):
+        b, low, high = CHUNKS[n]
         return pltpu.make_async_copy(
-            basis.at[batch, pl.ds(pl.multiple_of(block * BLOCK, BLOCK), BLOCK), pl.ds(place, TILE)],
-            phi.at[slot, :, pl.ds(j * TILE, TILE)],
-            sems.at[slot, j],
+            outgoing.at[b, me, pl.ds(low, high - low)], arrived[n].at[me], here_sems.at[n]
         )
 
-    for j in range(KT + 3):
-        fetch(0, 0, j).start()
-
-    for t in range(KT):
-        turn = lax.shift_right_arithmetic(start + t, 4)
-        for kind in range(4):
-            live = (info[10 + t] * info[10 + (t + kind) % KT]).astype(F32)
-            for m in range(2):
-                q = lax.bitwise_and(kind + 4 * m + turn, 7)
-                value = decode(arrived[:, q, t]).reshape(TILE, TILE) * live
-                high = value.astype(BF16)
-                low = (value - high.astype(F32)).astype(BF16)
-                columns = pl.ds(m * TILE, TILE)
-                matrix[t, pl.ds(kind * TILE, TILE), columns] = high
-                matrix[t, pl.ds((4 + kind) * TILE, TILE), columns] = low
-
-    dens[...] = jnp.zeros(dens.shape, F32)
-
-    def step(block, carry):
-        slot = lax.bitwise_and(block, 1)
-
-        @pl.when(block + 1 < blocks)
-        def _():
-            for j in range(KT + 3):
-                fetch(block + 1, 1 - slot, j).start()
-
-        for j in range(KT + 3):
-            fetch(block, slot, j).wait()
-        total = jnp.zeros((BLOCK, 2 * TILE), F32)
-        for t in range(KT):
-            left = phi[slot, :, pl.ds(t * TILE, 4 * TILE)]
-            product = jnp.dot(
-                left, matrix[t, pl.ds(0, 4 * TILE), :], preferred_element_type=F32
-            ) + jnp.dot(left, matrix[t, pl.ds(4 * TILE, 4 * TILE), :], preferred_element_type=F32)
-            own = left[:, :TILE].astype(F32)
-            total = total + product * jnp.concatenate([own, own], axis=1)
-        for m in range(2):
-            for i in range(GROUPS):
-                part = total[i * TILE : (i + 1) * TILE, m * TILE : (m + 1) * TILE]
-                dens[m, pl.ds(block * GROUPS + i, 1), :] = jnp.sum(part.T, axis=0, keepdims=True)
-        return carry
-
-    lax.fori_loop(0, blocks, step, 0)
-
-    rows = dens.shape[1]
+    def basis_copy(b, j):
+        return pltpu.make_async_copy(
+            basis.at[b, :, pl.ds(j * TILE, TILE)], values[b].at[j], basis_sems.at[b, j]
+        )
+
+    for n, (b, low, high) in enumerate(CHUNKS):
+
+        def send(i, carry, n=n, b=b, low=low, high=high):
+            to = partner(spot, i)
+            pltpu.make_async_remote_copy(
+                src_ref=outgoing.at[b, flat(to), pl.ds(low, high - low)],
+                dst_ref=arrived[n].at[me],
+                send_sem=send_sems.at[n],
+                recv_sem=recv_sems.at[n],
+                device_id=tuple(to),
+                device_id_type=MESH_ID,
+            ).start()
+            return carry
+
+        lax.fori_loop(1, DEVS, send, 0)
+        own_copy(n).start()
+        if n < 2:
+            for j in range(KT):
+                basis_copy(n, j).start()
+
+    others = pl.ds(0, DEVS - 1)
+    rows = points // TILE
     place = lax.broadcasted_iota(I32, (rows, TILE), 0) * TILE + lax.broadcasted_iota(
         I32, (rows, TILE), 1
     )
-    inside = place < count
-    harmonic = harmonics(offsets[0], offsets[1], offsets[2])
-    weight = weights[...]
-    factors = [weight] + [weight * item for item in harmonic[1:]]
-    hits = [atoms[...] == lax.bitwise_and(base + j, ATOMS - 1) for j in range(8)]
-    sums[...] = jnp.zeros(sums.shape, F32)
-    for m in range(2):
-        value = jnp.where(inside, dens[m], 0.0)
-        dens[m] = value
-        for h in range(9):
-            term = value * factors[h]
-            for j in range(8):
-                picked = jnp.where(hits[j], term, 0.0)
-                sums[pl.ds(j * 18 + m * 9 + h, 1), :] = jnp.sum(picked, axis=0, keepdims=True)
-    for i in range(2):
-        part = sums[pl.ds(i * TILE, TILE), :]
-        moments[pl.ds(i, 1), :] = jnp.sum(part.T, axis=0, keepdims=True)
-
-
-def batch_density(batch, info, arrived, basis, offsets, weights, atoms):
+    for n, (b, low, high) in enumerate(CHUNKS):
+        first = low == 0
+        last = high == KT
+        if first:
+            for j in range(KT):
+                basis_copy(b, j).wait()
+        own_copy(n).wait()
+        wait_all(arrived[n].at[others], recv_sems.at[n])
+        for t in range(low, high):
+            turn = lax.shift_right_arithmetic(info[b, 0] + t, 4)
+            for kind in range(4):
+                live = (info[b, 3 + KT + t] * info[b, 3 + KT + (t + kind) % KT]).astype(F32)
+                for m in range(2):
+                    q = lax.bitwise_and(kind + 4 * m + turn, 7)
+                    codes = [arrived[n][s * N_COL + q, t - low] for s in range(N_ROW)]
+                    value = decode(jnp.concatenate(codes, axis=0)) * live
+                    upper = value.astype(BF16)
+                    lower = (value - upper.astype(F32)).astype(BF16)
+                    columns = pl.ds(m * TILE, TILE)
+                    matrix[t, pl.ds(kind * TILE, TILE), columns] = upper
+                    matrix[t, pl.ds((4 + kind) * TILE, TILE), columns] = lower
+        at = [info[b, 3 + t] for t in range(KT)]
+
+        def step(block, carry, b=b, low=low, high=high, first=first, last=last, at=at):
+            span = pl.ds(pl.multiple_of(block * BLOCK, BLOCK), BLOCK)
+            total = None if first else kept[span, :]
+            for t in range(low, high):
+                left = jnp.concatenate(
+                    [values[b][at[(t + i) % KT], span, :] for i in range(4)], axis=1
+                )
+                product = jnp.dot(
+                    left, matrix[t, pl.ds(0, 4 * TILE), :], preferred_element_type=F32
+                ) + jnp.dot(
+                    left, matrix[t, pl.ds(4 * TILE, 4 * TILE), :], preferred_element_type=F32
+                )
+                own = left[:, :TILE].astype(F32)
+                term = product * jnp.concatenate([own, own], axis=1)
+                total = term if total is None else total + term
+            if not last:
+                kept[span, :] = total
+            else:
+                for m in range(2):
+                    for i in range(GROUPS):
+                        part = total[i * TILE : (i + 1) * TILE, m * TILE : (m + 1) * TILE]
+                        dens[m, b, pl.ds(block * GROUPS + i, 1), :] = jnp.sum(
+                            part.T, axis=0, keepdims=True
+                        )
+            return carry
+
+        lax.fori_loop(0, points // BLOCK, step, 0)
+        if not last:
+            continue
+        inside = place < info[b, 1]
+        harmonic = harmonics(offsets[0, b], offsets[1, b], offsets[2, b])
+        weight = weights[b]
+        factors = [weight] + [weight * item for item in harmonic[1:]]
+        atom = atoms[b]
+        hits = [atom == lax.bitwise_and(info[b, 2] + j, ATOMS - 1) for j in range(8)]
+        sums[...] = jnp.zeros(sums.shape, F32)
+        for m in range(2):
+            value = jnp.where(inside, dens[m, b], 0.0)
+            dens[m, b] = value
+            for h in range(9):
+                term = value * factors[h]
+                for j in range(8):
+                    picked = jnp.where(hits[j], term, 0.0)
+                    sums[pl.ds(j * 18 + m * 9 + h, 1), :] = jnp.sum(
+                        picked, axis=0, keepdims=True
+                    )
+        for i in range(2):
+            part = sums[pl.ds(i * TILE, TILE), :]
+            moments[b, pl.ds(i, 1), :] = jnp.sum(part.T, axis=0, keepdims=True)
+    for n in range(len(CHUNKS)):
+        wait_all(arrived[n].at[others], send_sems.at[n])
+
+
+def batches(info, outgoing, basis, offsets, weights, atoms):
     points = basis.shape[1]
     rows = points // TILE
     return pl.pallas_call(
-        functools.partial(batch_kernel, batch),
-        name="batch_density",
+        batches_kernel,
+        name="batches",
         out_shape=(
-            jax.ShapeDtypeStruct((2, rows, TILE), F32),
-            jax.ShapeDtypeStruct((2, TILE), F32),
+            jax.ShapeDtypeStruct((2, 2, rows, TILE), F32),
+            jax.ShapeDtypeStruct((2, 2, TILE), F32),
         ),
-        in_specs=[SMEM_SPEC, VMEM_SPEC, ANY_SPEC, VMEM_SPEC, VMEM_SPEC, VMEM_SPEC],
+        in_specs=[SMEM_SPEC, ANY_SPEC, ANY_SPEC, VMEM_SPEC, VMEM_SPEC, VMEM_SPEC],
         out_specs=(VMEM_SPEC, VMEM_SPEC),
         scratch_shapes=[
+            *(pltpu.VMEM((DEVS, high - low, 8, TILE), I16) for _, low, high in CHUNKS),
+            pltpu.VMEM((KT, points, TILE), BF16),
+            pltpu.VMEM((KT, points, TILE), BF16),
             pltpu.VMEM((KT, 8 * TILE, 2 * TILE), BF16),
-            pltpu.VMEM((2, BLOCK, (KT + 3) * TILE), BF16),
+            pltpu.VMEM((points, 2 * TILE), F32),
             pltpu.VMEM((2 * TILE, TILE), F32),
-            pltpu.SemaphoreType.DMA((2, KT + 3)),
+            pltpu.SemaphoreType.DMA((len(CHUNKS),)),
+            pltpu.SemaphoreType.DMA((len(CHUNKS),)),
+            pltpu.SemaphoreType.DMA((len(CHUNKS),)),
+            pltpu.SemaphoreType.DMA((2, KT)),
         ],
-        compiler_params=pltpu.CompilerParams(vmem_limit_bytes=VMEM_LIMIT),
-        cost_estimate=pl.CostEstimate(
-            flops=2 * points * 1024 * 256 * KT, bytes_accessed=12_000_000, transcendentals=0
-        ),
-    )(info, arrived, basis, offsets, weights, atoms)
-
-
-def exchange(value):
-    return lax.all_to_all(value, ROW_COL, split_axis=0, concat_axis=0, tiled=True)
+        compiler_params=pltpu.CompilerParams(has_side_effects=True, vmem_limit_bytes=VMEM_LIMIT),
+    )(info, outgoing, basis, offsets, weights, atoms)
 
 
 def local(
@@ -311,41 +466,31 @@
     device = my_row * N_COL + my_col
     meta = jnp.stack([my_row, my_col])
     own_start = jnp.min(tile_list, axis=1)
-    starts = exchange(jnp.broadcast_to(own_start[None], (DEVS, 2))).reshape(-1)
-
-    slices = extract(meta, density_first, density_second)
-    slices = exchange(slices.reshape(DEVS, 2, 2, 8, TILE))
-    outgoing = pack(meta, starts, slices)
-    arrived = [exchange(outgoing[b]) for b in range(2)]
-
     place = jnp.argsort(tile_list, axis=1).astype(I32)
     live = (place < tile_count[:, None]).astype(I32)
     base = (2 * device + jnp.arange(2, dtype=I32)) * 4 % ATOMS
     info = jnp.concatenate(
         [own_start[:, None], point_count[:, None], base[:, None], place, live], axis=1
     )
-    dens = []
-    moments = []
-    for b in range(2):
-        one, part = batch_density(
-            b,
-            info[b],
-            arrived[b].reshape(N_ROW, N_COL, KT, 8, TILE),
-            basis,
-            offsets[:, b].reshape(3, rows, TILE),
-            weights[b].reshape(rows, TILE),
-            atom_of_point[b].reshape(rows, TILE),
-        )
-        dens.append(one.reshape(2, points))
-        moments.append(part.reshape(-1)[: 8 * 18])
-    density = jnp.stack(dens, axis=1)
+    offsets = offsets.reshape(3, 2, rows, TILE)
+    weights = weights.reshape(2, rows, TILE)
+    atom_of_point = atom_of_point.reshape(2, rows, TILE)
+
+    slices = extract(meta, density_first, density_second)
+    slices, starts = spread(
+        slices.reshape(DEVS, 2, 2, 8, TILE), jnp.pad(own_start, (0, TILE - 2))[None]
+    )
+    outgoing = pack(meta, starts[:, 0, :2].reshape(-1), slices)
+    dens, moments = batches(info, outgoing, basis, offsets, weights, atom_of_point)
+    density = dens.reshape(2, 2, points)
+    moments = moments.reshape(2, -1)[:, : 8 * 18]
     half = 4 * 18
     own = jnp.concatenate(
         [moments[0][:half], moments[0][half:] + moments[1][:half], moments[1][half:]]
     )
     spare = jnp.zeros((2 * TILE - 3 * half,), F32)
     own = jnp.concatenate([own, spare])
-    everyone = exchange(jnp.broadcast_to(own[None], (DEVS, 2 * TILE)))
+    everyone = share(own[None])[:, 0]
     main = everyone[:, : 2 * half]
     extra = jnp.roll(everyone[:, 2 * half : 3 * half], 1, axis=0)
     whole = main + jnp.concatenate([extra, jnp.zeros_like(extra)], axis=1)

time: 169 us -> 161 us (0.953)
  Pallas kernels: 46.3 us -> 145 us
  waiting for transfers between devices: 63.2 us -> 0 us
  starting transfers between devices: 37.9 us -> 0 us
  local copies, waits for them, and re-layouts: 13.7 us -> 10.9 us
    pallas_call x2 -> x3, Pallas kernels: 35.1 us -> 134 us  [the longest x1 76.2 us: batches(): pl.pallas_call(batches_kernel, name='batches', out_shape=(jax.ShapeDtypeS...]
    all_to_all x5 -> x0, waiting for transfers between devices: 63.2 us -> none  [exchange(): lax.all_to_all(value, ROW_COL, split_axis=0, concat_axis=0, tiled=True)]
    all_to_all x5 -> x0, starting transfers between devices: 37.9 us -> none  [exchange(): lax.all_to_all(value, ROW_COL, split_axis=0, concat_axis=0, tiled=True)]
    squeeze x2 -> x0, local copies, waits for them, and re-layouts: 5.06 us -> none  [the longest x1 4.47 us: local(): arrived = [exchange(outgoing[b]) for b in range(2)]]
    unnamed x23 -> x12, local copies, waits for them, and re-layouts: 3.07 us -> 4.31 us
  transfers between devices with their start and end apart: 5 -> 0, of which waited for: 5 -> 0; matrix products, arithmetic and copies ran while one was open for 5% -> 0% of each run, Pallas kernels for 13% -> 0%
where the time goes in v1:
time: 161 us; the launch traced here: 160 us
  Pallas kernels  145 us (90%)
  local copies, waits for them, and re-layouts  10.9 us (7%)
  other arithmetic  3.59 us (2%)
    pallas_call x1, Pallas kernels, batches(): pl.pallas_call(batches_kernel, name='batches', out_shape=(jax.ShapeDtypeS...  76.2 us
    pallas_call x1, Pallas kernels, spread(): pl.pallas_call(spread_kernel, name='spread', out_shape=(jax.ShapeDtypeStr...  35.9 us
    pallas_call x1, Pallas kernels, share(): pl.pallas_call(share_kernel, name='share', out_shape=jax.ShapeDtypeStruct...  21.8 us
    pallas_call x1, Pallas kernels, pack(): pl.pallas_call(pack_kernel, name='pack', out_shape=jax.ShapeDtypeStruct((...  6.14 us
    pallas_call x1, Pallas kernels, extract(): pl.pallas_call(extract_kernel, name='extract', out_shape=jax.ShapeDtypeSt...  5.12 us
    unnamed x12, local copies, waits for them, and re-layouts  4.31 us

profile of v1, /device:TPU:1, one launch (start us, length us, event | category | flops | bytes accessed | tf_op | source)
XLA Modules:
  0.0 160.5 jit_solution(13551175762379011929)
XLA Ops:
  0.6 0.8 reduce_min.9
  1.4 0.1 copy.15
  1.5 0.7 copy.16
  2.3 0.8 copy.13
  3.0 0.7 sort.17
  3.7 0.1 copy.17
  3.8 0.7 compare_convert_fusion
  4.5 0.7 concatenate.13.info
  5.2 0.7 pad_add_fusion.meta
  5.8 5.1 %extract.1 = bf16[16,8,2,2,8,128]{5,4,3,2,1,0:T(8,128)(2,1)} custom-call(s32[2]{0:T(128)} %pad_add_fusion.meta, bf16[768,1536]{1,0:T(8,128)(2,1)} %first.1, bf16[768,1536]{1,0:T(8,128)(2,1)} %second.1), custom_call_target="tpu_custom_call" | custom-call | tf_op jit(solution)/shard_map/extract/pallas_call | solution.py:74
  11.0 0.0 copy-start
  11.0 0.0 copy-start.1
  11.0 0.0 copy-start.2
  11.0 0.5 pad_bitcast_fusion.own
  11.5 35.9 %spread.1 = (bf16[128,2,2,8,128]{4,3,2,1,0:T(8,128)(2,1)}, s32[128,1,128]{2,1,0:T(1,128)}) custom-call(bf16[128,2,2,8,128]{4,3,2,1,0:T(8,128)(2,1)} %bitcast.32, s32[1,128]{1,0:T(1,128)} %pad_bitcast_fusion.own), custom_call_target="tpu_custom_call" | custom-call | tf_op jit(solution)/shard_map/spread/pallas_call | solution.py:173
  47.4 1.0 slice_reduce_fusion
  48.4 0.7 reshape_squeeze.3.starts
  49.1 6.1 %pack.1.outgoing = s16[2,128,7,8,128]{4,3,2,1,0:T(8,128)(2,1)} custom-call(s32[2]{0:T(128)} %pad_add_fusion.meta, s32[256]{0:T(256)} %reshape_squeeze.3.starts, bf16[128,2,2,8,128]{4,3,2,1,0:T(8,128)(2,1)} %get-tuple-element.9.slices), custom_call_target="tpu_custom_call" | custom-call | tf_op jit(solution)/shard_map/pack/pallas_call | solution.py:270
  55.3 0.0 copy-done
  55.3 0.7 reshape.78.offsets
  56.0 0.0 copy-done.1
  56.0 0.6 copy.30
  56.6 0.0 copy-done.2
  56.6 0.6 copy.29
  57.3 76.2 %batches.1 = (f32[2,2,32,128]{3,2,1,0:T(8,128)}, f32[2,2,128]{2,1,0:T(2,128)}) custom-call(s32[2,17]{1,0:T(2,128)} %concatenate.13.info, s16[2,128,7,8,128]{4,3,2,1,0:T(8,128)(2,1)} %pack.1.outgoing, bf16[2,4096,896]{2,1,0:T(8,128)(2,1)} %basis.1, f32[3,2,32,128]{3,2,1,0:T(8,128)} %reshape.78.offsets, f32[2,32,128]{2,1,0:T(8,128)} %bitcast.37, ...), custom_call_target="tpu_custom_call" | custom-call | tf_op jit(solution)/shard_map/batches/pallas_call | solution.py:426
  133.5 1.5 reshape.81
  135.0 0.7 copy.31
  135.7 0.1 slice_bitcast_fusion.1
  135.8 0.6 pad_maximum_fusion
  136.4 21.8 %share.1 = f32[128,1,256]{2,1,0:T(1,128)} custom-call(f32[1,256]{1,0:T(1,128)} %bitcast.42), custom_call_target="tpu_custom_call" | custom-call | tf_op jit(solution)/shard_map/share/pallas_call | solution.py:214
  158.3 0.9 copy.28
  159.2 0.1 slice.64
  159.2 0.1 slice.63
  159.4 0.2 reshape.83
  159.6 0.2 copy.18
  159.8 0.7 copy.19
  (5 shorter events, 0.1 us)
Async XLA Ops:
  11.0 44.3 %copy-start = (f32[3,2,4096]{2,1,0:T(2,128)S(1)}, f32[3,2,4096]{2,1,0:T(2,128)}, u32[]{:S(2)}) copy-start(f32[3,2,4096]{2,1,0:T(2,128)} %param.15) | copy-start | bytes 294916
  11.0 45.1 %copy-start.1 = (f32[2,4096]{1,0:T(2,128)S(1)}, f32[2,4096]{1,0:T(2,128)}, u32[]{:S(2)}) copy-start(f32[2,4096]{1,0:T(2,128)} %param.16) | copy-start | bytes 98308
  11.0 45.7 %copy-start.2 = (s32[2,4096]{1,0:T(2,128)S(1)}, s32[2,4096]{1,0:T(2,128)}, u32[]{:S(2)}) copy-start(s32[2,4096]{1,0:T(2,128)} %param.17) | copy-start | bytes 98308
